TPU v7x, 32 devices: a whole 2x2x4 slice. The times are simulated.
32 devices in a mesh: cfg: 2 (over y), gx: 8 (over z, x), gy: 2 (over core).
Axes of the slice: x: 2, y: 2, z: 4, core: 2. Of those that a mesh axis runs over, the one named last changes fastest.
Arguments:
- gauge_links: float32 [4, 12, 16, 16, 1024], P(None, None, ('cfg', 'gx'), 'gy'), parts along dimension 2, may hold values from -1 to 1, as said below
- momentum: float32 [8, 16, 16, 1024], P(None, ('cfg', 'gx'), 'gy'), parts along dimension 1, may hold values from -6 to 6
Outputs:
- new_momentum: float32 [8, 16, 16, 1024], P(None, ('cfg', 'gx'), 'gy'), parts along dimension 1
- new_link: float32 [12, 16, 16, 1024], P(None, ('cfg', 'gx'), 'gy'), parts along dimension 1
There are 2 independent parts, one for each index of `cfg`. A program takes and returns all parts, laid end to end along the dimension named above; each array names one. Nothing has to cross between parts.
Inputs may be any that keep to these rules, and one draw needn't show every extreme that they name: `gauge_links`: for every direction and site the two rows are orthonormal complex 3-vectors up to rounding.
All inputs are finite; a program needn't handle non-finite values.
Results may differ from a plain program's by a relative error of at most 0.0003.
Values sent between devices are 32-bit elements; how exact they have to be, the bound alone decides.
A program may use at most 128 MiB of HBM per device.

v0:
```python
import math

import jax
import jax.numpy as jnp
import numpy as np
from jax import lax
from jax.experimental import pallas as pl
from jax.experimental.pallas import tpu as pltpu
from jax.sharding import PartitionSpec as P

NZ = 32
NT = 32

coupling = 6.0
step_force = 0.3
step_link = 0.15
kernel_mass = 0.01

LANES = 128


def hartley(length):
    index = np.arange(length)
    angle = (index[:, None] * index[None, :] % length) * (2.0 * math.pi / length)
    return (np.cos(angle) + np.sin(angle)) / math.sqrt(length)


def sine_squares(length):
    return np.sin(np.arange(length) * (math.pi / length)) ** 2


def tables(x_total, y_total, count, parts):
    mix_xy = np.kron(hartley(x_total), hartley(y_total)).astype(np.float32)
    row_part = 4.0 * (sine_squares(x_total)[:, None] + sine_squares(y_total)[None, :])
    row_part = (kernel_mass + row_part).reshape(-1, 1).astype(np.float32)
    plane = 4.0 * (sine_squares(NZ)[:, None] + sine_squares(NT)[None, :]).reshape(-1)
    plane = np.tile(plane, count).reshape(parts, 1, -1).astype(np.float32)
    z_rows = np.repeat(hartley(NZ), NT, axis=1).reshape(NZ, 1, NZ * NT).astype(np.float32)
    t_rows = np.tile(hartley(NT), (1, NZ)).astype(np.float32)
    return mix_xy, row_part, plane, z_rows, t_rows


def cmul_sum(terms):
    real, imag = None, None
    for (a, b), (c, d) in terms:
        re = a * c - b * d
        im = a * d + b * c
        real = re if real is None else real + re
        imag = im if imag is None else imag + im
    return (real, imag)


def product(left, right):
    return [
        [cmul_sum([(left[i][m], right[m][k]) for m in range(3)]) for k in range(len(right[0]))]
        for i in range(len(left))
    ]


def adjoint(matrix):
    return [[(matrix[k][i][0], -matrix[k][i][1]) for k in range(3)] for i in range(3)]


def third_row(rows):
    third = []
    for column in range(3):
        j, k = (column + 1) % 3, (column + 2) % 3
        (ar, ai), (br, bi) = rows[0][j], rows[1][k]
        (cr, ci), (dr, di) = rows[0][k], rows[1][j]
        third.append((ar * br - ai * bi - (cr * dr - ci * di), -(ar * bi + ai * br - (cr * di + ci * dr))))
    return [rows[0], rows[1], third]


def load_link(ref, lanes):
    rows = [[(ref[3 * r + k, :, lanes], ref[6 + 3 * r + k, :, lanes]) for k in range(3)] for r in range(2)]
    return third_row(rows)


def algebra_parts(left, right):
    full = product(left, right)

    def re(i, k):
        return full[i][k][0]

    def im(i, k):
        return full[i][k][1]

    return [
        im(1, 0) + im(0, 1),
        re(0, 1) - re(1, 0),
        im(0, 0) - im(1, 1),
        im(2, 0) + im(0, 2),
        re(0, 2) - re(2, 0),
        im(2, 1) + im(1, 2),
        re(1, 2) - re(2, 1),
        (im(0, 0) + im(1, 1) - 2.0 * im(2, 2)) * (1.0 / math.sqrt(3.0)),
    ]


def square(c, p, q):
    c0, c1, c2 = c

    def mul(a, b):
        return (a[0] * b[0] - a[1] * b[1], a[0] * b[1] + a[1] * b[0])

    def sq(a):
        return (a[0] * a[0] - a[1] * a[1], 2.0 * (a[0] * a[1]))

    c01, c02, c12 = mul(c0, c1), mul(c0, c2), mul(c1, c2)
    s0, s1, s2 = sq(c0), sq(c1), sq(c2)
    return [
        tuple(s0[i] + 2.0 * (c12[i] * q) for i in range(2)),
        tuple(2.0 * (c01[i] + c12[i] * p) + s2[i] * q for i in range(2)),
        tuple(s1[i] + 2.0 * c02[i] + s2[i] * p for i in range(2)),
    ]


def rotation_rows(parts):
    scale = 0.25 * step_link
    root_inv = 1.0 / math.sqrt(3.0)
    g = [0.5 * scale * part for part in parts]
    g8 = root_inv * g[7]
    b00, b11, b22 = g8 + g[2], g8 - g[2], -2.0 * g8
    b01, b02, b12 = (g[0], -g[1]), (g[3], -g[4]), (g[5], -g[6])

    def norm(a):
        return a[0] * a[0] + a[1] * a[1]

    n01, n02, n12 = norm(b01), norm(b02), norm(b12)
    d00, d11 = b00 * b00 + n01 + n02, b11 * b11 + n01 + n12
    p = 0.5 * (b00 * b00 + b11 * b11 + b22 * b22) + n01 + n02 + n12
    t_re = b01[0] * b12[0] - b01[1] * b12[1]
    t_im = b01[0] * b12[1] + b01[1] * b12[0]
    q = b00 * b11 * b22 + 2.0 * (t_re * b02[0] + t_im * b02[1]) - b00 * n12 - b11 * n02 - b22 * n01
    e01 = (b01[0] * (b00 + b11) + b02[0] * b12[0] + b02[1] * b12[1],
           b01[1] * (b00 + b11) + b02[1] * b12[0] - b02[0] * b12[1])
    e02 = (b02[0] * (b00 + b22) + t_re, b02[1] * (b00 + b22) + t_im)
    e12 = (b12[0] * (b11 + b22) + b01[0] * b02[0] + b01[1] * b02[1],
           b12[1] * (b11 + b22) + b01[0] * b02[1] - b01[1] * b02[0])
    p2, pq = p * p, p * q
    c = [
        (1.0 - q * q * (1.0 / 720), pq * (1.0 / 120) - q * (1.0 / 6)),
        (q * (1.0 / 24) - pq * (1.0 / 360), 1.0 - p * (1.0 / 6) + p2 * (1.0 / 120)),
        (p * (1.0 / 24) - 0.5 - p2 * (1.0 / 720), q * (1.0 / 120)),
    ]
    c = square(square(c, p, q), p, q)
    c0, c1, c2 = c

    def diag(b, d):
        return tuple(c0[i] + c1[i] * b + c2[i] * d for i in range(2))

    def off(b, d, sign):
        bi, di = (b[1], d[1]) if sign > 0 else (-b[1], -d[1])
        return (
            c1[0] * b[0] - c1[1] * bi + c2[0] * d[0] - c2[1] * di,
            c1[0] * bi + c1[1] * b[0] + c2[0] * di + c2[1] * d[0],
        )

    return [
        [diag(b00, d00), off(b01, e01, 1), off(b02, e02, 1)],
        [off(b01, e01, -1), diag(b11, d11), off(b12, e12, 1)],
    ]


def split(value):
    high = value.astype(jnp.bfloat16)
    return high, (value - high.astype(jnp.float32)).astype(jnp.bfloat16)


def plane_transform(value, high_ref, low_ref):
    rows = value.shape[0]
    high, low = split(value)
    both = jnp.dot(jnp.concatenate([high, low], axis=0), high_ref[...], preferred_element_type=jnp.float32)
    rest = jnp.dot(high, low_ref[...], preferred_element_type=jnp.float32)
    return both[:rows] + both[rows:] + rest


def move_z(value, steps):
    return pltpu.roll(value, (steps * NT) % value.shape[1], 1)


def move_t(value, steps):
    lanes = value.shape[1]
    inside = pltpu.roll(value, steps % lanes, 1)
    beside = pltpu.roll(value, (steps - steps * NT) % lanes, 1)
    t_index = lax.broadcasted_iota(jnp.int32, value.shape, 1) % NT
    wraps = jnp.logical_or(t_index - steps < 0, t_index - steps >= NT)
    return jnp.where(wraps, beside, inside)


def move_y(value, beyond, steps):
    rows = value.shape[0]
    row_index = lax.broadcasted_iota(jnp.int32, value.shape, 0)
    edge = row_index == (0 if steps > 0 else rows - 1)
    shift = steps % rows
    return jnp.where(edge, pltpu.roll(beyond, shift, 0), pltpu.roll(value, shift, 0))


def step_kernel(
    gx_count, gy_count,
    links, momentum, mix_xy, row_part, plane, z_rows, t_rows,
    out_momentum, out_link,
    ahead, peer_x, shifted_x, lower, peer_lower, total,
    outgoing, gathered, filtered, returned, table_high, table_low, weights,
    halo_send, halo_recv, peer_send, peer_recv, out_send, out_recv, back_send, back_recv,
):
    gx, gy = lax.axis_index("gx"), lax.axis_index("gy")
    parts = gx_count * gy_count
    me = gx * gy_count + gy
    colors, rows, sites = momentum.shape
    width = outgoing.shape[2]
    chunks = sites // LANES
    behind = {"gx": lax.rem(gx + gx_count - 1, gx_count), "gy": gy}
    y_after = {"gx": gx, "gy": lax.rem(gy + 1, gy_count)}
    y_before = {"gx": gx, "gy": lax.rem(gy + gy_count - 1, gy_count)}

    def place(index):
        return {"gx": index // gy_count, "gy": lax.rem(index, gy_count)}

    barrier = pltpu.get_barrier_semaphore()

    def greet(offset, carry):
        pl.semaphore_signal(barrier, inc=1, device_id=place(lax.rem(me + offset, parts)))
        return carry

    lax.fori_loop(1, parts, greet, 0)
    pl.semaphore_wait(barrier, parts - 1)

    halo = [
        pltpu.make_async_remote_copy(
            links.at[nu + 1], ahead.at[nu], halo_send.at[nu], halo_recv.at[nu], device_id=behind
        )
        for nu in range(3)
    ]
    fetch_x = pltpu.make_async_remote_copy(
        links.at[0], peer_x, peer_send.at[0], peer_recv.at[0], device_id=y_before
    )
    fetch_x.start()
    for copy in halo:
        copy.start()

    def make_table(z, carry):
        block = t_rows[...] * z_rows[z]
        high, low = split(block)
        at = pl.ds(pl.multiple_of(z * NT, NT), NT)
        table_high[at, :] = high
        table_low[at, :] = low
        return carry

    lax.fori_loop(0, NZ, make_table, 0)
    weights[...] = 4.0 / (row_part[...] + plane[me])

    def shift_sides(entry, carry):
        value = links[0, entry]
        shifted_x[1, entry] = move_z(value, -1)
        shifted_x[2, entry] = move_t(value, -1)
        return carry

    lax.fori_loop(0, 12, shift_sides, 0)
    fetch_x.wait()

    def shift_y(entry, carry):
        shifted_x[0, entry] = move_y(links[0, entry], peer_x[entry], -1)
        return carry

    lax.fori_loop(0, 12, shift_y, 0)

    def direction(nu, first):
        def chunk(j, carry):
            lanes = pl.ds(pl.multiple_of(j * LANES, LANES), LANES)
            link_nu = load_link(links.at[nu + 1], lanes)
            across = load_link(shifted_x.at[nu], lanes)
            corner = product(load_link(links.at[0], lanes), load_link(ahead.at[nu], lanes))
            upper = algebra_parts(corner, adjoint(product(link_nu, across)))
            below = algebra_parts(product(across, adjoint(corner)), link_nu)
            for a in range(8):
                total[a, :, lanes] = upper[a] if first else total[a, :, lanes] + upper[a]
                lower[nu, a, :, lanes] = below[a]
            return carry

        lax.fori_loop(0, chunks, chunk, 0)

    halo[0].wait()
    direction(0, True)
    send_lower = pltpu.make_async_remote_copy(
        lower.at[0], peer_lower, peer_send.at[1], peer_recv.at[1], device_id=y_after
    )
    send_lower.start()
    halo[1].wait()
    direction(1, False)
    send_lower.wait()
    halo[2].wait()
    direction(2, False)

    def finish(a, carry):
        force = total[a] + move_z(lower[1, a], 1) + move_t(lower[2, a], 1)
        force = force + move_y(lower[0, a], peer_lower[a], 1)
        out_momentum[a] = momentum[a] - (step_force * coupling / 6.0) * force
        return carry

    lax.fori_loop(0, 8, finish, 0)

    spectrum = plane_transform(out_momentum[...].reshape(colors * rows, sites), table_high, table_low)
    spectrum = spectrum.reshape(colors, rows, sites)
    pieces = sites // width
    for part in range(parts):
        c, k = part // pieces, part % pieces
        outgoing[part] = spectrum[c, :, k * width : (k + 1) * width]

    def own_rows(index):
        return pl.ds(pl.multiple_of(index * rows, rows), rows)

    def out_copy(to, source):
        return pltpu.make_async_remote_copy(
            outgoing.at[to], gathered.at[own_rows(source)], out_send.at[to], out_recv.at[source],
            device_id=place(to),
        )

    def start_out(offset, carry):
        out_copy(lax.rem(me + offset, parts), me).start()
        return carry

    def wait_out(offset, carry):
        other = lax.rem(me + offset, parts)
        out_copy(other, other).wait()
        return carry

    lax.fori_loop(1, parts, start_out, 0)
    gathered[own_rows(me), :] = outgoing[me]
    lax.fori_loop(1, parts, wait_out, 0)

    def mix(source, target, weighted):
        total_rows = mix_xy.shape[0]
        size = min(total_rows, LANES)

        def block(index, carry):
            at = pl.ds(pl.multiple_of(index * size, size), size)
            mixed = jnp.dot(
                mix_xy[at, :], source[...], preferred_element_type=jnp.float32,
                precision=lax.Precision.HIGHEST,
            )
            target[at, :] = mixed * weights[at, :] if weighted else mixed
            return carry

        lax.fori_loop(0, total_rows // size, block, 0)

    mix(gathered, filtered, True)
    mix(filtered, gathered, False)

    def back_copy(to, source):
        return pltpu.make_async_remote_copy(
            gathered.at[own_rows(to)], returned.at[source], back_send.at[to], back_recv.at[source],
            device_id=place(to),
        )

    def start_back(offset, carry):
        back_copy(lax.rem(me + offset, parts), me).start()
        return carry

    def wait_back(offset, carry):
        other = lax.rem(me + offset, parts)
        back_copy(other, other).wait()
        return carry

    lax.fori_loop(1, parts, start_back, 0)
    returned[me] = gathered[own_rows(me), :]
    lax.fori_loop(1, parts, wait_back, 0)

    back = jnp.concatenate(
        [
            jnp.concatenate([returned[c * pieces + k] for k in range(pieces)], axis=1)
            for c in range(colors)
        ],
        axis=0,
    )
    total[...] = plane_transform(back, table_high, table_low).reshape(colors, rows, sites)

    def update(j, carry):
        lanes = pl.ds(pl.multiple_of(j * LANES, LANES), LANES)
        rotation = rotation_rows([total[a, :, lanes] for a in range(8)])
        updated = product(rotation, load_link(links.at[0], lanes))
        for r in range(2):
            for k in range(3):
                out_link[3 * r + k, :, lanes] = updated[r][k][0]
                out_link[6 + 3 * r + k, :, lanes] = updated[r][k][1]
        return carry

    lax.fori_loop(0, chunks, update, 0)


def shards(gauge_links, momentum):
    gx_count, gy_count = lax.axis_size("gx"), lax.axis_size("gy")
    colors, layers, rows, sites = momentum.shape
    assert layers == 1
    parts = gx_count * gy_count
    width = colors * sites // parts
    assert sites % width == 0
    links = gauge_links.reshape(4, 12, rows, sites)
    fields = momentum.reshape(colors, rows, sites)
    f32 = jnp.float32
    everything = rows * parts
    dma = pltpu.SemaphoreType.DMA

    def body(*refs):
        step_kernel(gx_count, gy_count, *refs)

    vmem = pl.BlockSpec(memory_space=pltpu.VMEM)
    new_momentum, new_link = pl.pallas_call(
        body,
        out_shape=(
            jax.ShapeDtypeStruct((colors, rows, sites), f32),
            jax.ShapeDtypeStruct((12, rows, sites), f32),
        ),
        in_specs=[vmem] * 7,
        out_specs=(vmem, vmem),
        scratch_shapes=[
            pltpu.VMEM((3, 12, rows, sites), f32),
            pltpu.VMEM((12, rows, sites), f32),
            pltpu.VMEM((3, 12, rows, sites), f32),
            pltpu.VMEM((3, colors, rows, sites), f32),
            pltpu.VMEM((colors, rows, sites), f32),
            pltpu.VMEM((colors, rows, sites), f32),
            pltpu.VMEM((parts, rows, width), f32),
            pltpu.VMEM((everything, width), f32),
            pltpu.VMEM((everything, width), f32),
            pltpu.VMEM((parts, rows, width), f32),
            pltpu.VMEM((sites, sites), jnp.bfloat16),
            pltpu.VMEM((sites, sites), jnp.bfloat16),
            pltpu.VMEM((everything, width), f32),
            dma((3,)), dma((3,)), dma((2,)), dma((2,)),
            dma((parts,)), dma((parts,)), dma((parts,)), dma((parts,)),
        ],
        compiler_params=pltpu.CompilerParams(
            collective_id=0, has_side_effects=True, vmem_limit_bytes=60 * 1024 * 1024
        ),
    )(links, fields, *tables(gx_count * layers, gy_count * rows, colors, parts))
    return (new_momentum.reshape(momentum.shape), new_link.reshape((12,) + momentum.shape[1:]))


def solution(mesh):
    return jax.shard_map(
        shards,
        mesh=mesh,
        in_specs=(P(None, None, ("cfg", "gx"), "gy", None), P(None, ("cfg", "gx"), "gy", None)),
        out_specs=(P(None, ("cfg", "gx"), "gy", None), P(None, ("cfg", "gx"), "gy", None)),
        check_vma=False,
    )
```

profile of v0, /device:TPU:0, one launch (start us, length us, event | category | flops | bytes accessed | tf_op | source)
XLA Modules:
  0.0 58.8 jit_solution(5030651268430078039)
XLA Ops:
  0.6 54.7 %shard_map.86 = (f32[8,8,1024]{2,1,0:T(8,128)}, f32[12,8,1024]{2,1,0:T(8,128)}) custom-call(f32[4,12,8,1024]{3,2,1,0:T(8,128)} %bitcast.8, f32[8,8,1024]{2,1,0:T(8,128)} %bitcast.10, f32[128,128]{1,0:T(8,128)} %constant.10.clone.refs_2_, f32[128,1]{1,0:T(8,128)} %constant.11.clone.refs_3_, f32[16,1,512]{2,1,0:T(1,128)} %constant.12.clone.refs_4_, ...), custom_call_target="tpu_custom_call" | custom-call | tf_op jit(solution)/shard_map/pallas_call | solution.py:408
  55.4 1.7 %copy.13 = f32[8,1,8,1024]{3,2,1,0:T(8,128)} copy(f32[8,1,8,1024]{3,2,1,0:T(8,128)} %bitcast.11) | data formatting | bytes 524288
  57.0 1.8 %copy.14 = f32[12,1,8,1024]{3,2,1,0:T(8,128)} copy(f32[12,1,8,1024]{3,2,1,0:T(8,128)} %bitcast.9) | data formatting | bytes 786432
where the time goes:
time: 59 us; the launch traced here: 58.8 us
  Pallas kernels  54.7 us (93%)
  local copies, waits for them, and re-layouts  3.44 us (6%)
  between operations  0.64 us (1%)
    pallas_call x1, Pallas kernels, shards(): pl.pallas_call(body, out_shape=(jax.ShapeDtypeStruct((colors, rows, sites...  54.7 us
    unnamed x2, local copies, waits for them, and re-layouts  3.44 us

commit v1 on v0

--- a/solution.py
+++ b/solution.py
@@ -17,6 +17,7 @@
 kernel_mass = 0.01
 
 LANES = 128
+HALVES = 2
 
 
 def hartley(length):
@@ -73,6 +74,33 @@
 
 def load_link(ref, lanes):
     rows = [[(ref[3 * r + k, :, lanes], ref[6 + 3 * r + k, :, lanes]) for k in range(3)] for r in range(2)]
+    return third_row(rows)
+
+
+def stereographic(pole, others):
+    size = sum(x * x for x in others[1:]) + others[0] * others[0]
+    south = pole < 0.0
+    factor = jnp.where(south, 1.0 - pole, 1.0) / jnp.where(south, jnp.maximum(size, 1e-24), 1.0 + pole)
+    out = [x * factor for x in others]
+    out[0] = jnp.where(jnp.logical_and(south, size < 1e-24), 1e12, out[0])
+    return out
+
+
+def encode(rows):
+    out = []
+    for row in rows:
+        out += stereographic(row[0][0], [row[0][1], row[1][0], row[1][1], row[2][0], row[2][1]])
+    return out
+
+
+def decode(values):
+    rows = []
+    for y in (values[:5], values[5:]):
+        n = sum(x * x for x in y[1:]) + y[0] * y[0]
+        near = 1.0 / (1.0 + n)
+        twice = 2.0 * near
+        u = [x * twice for x in y]
+        rows.append([((1.0 - n) * near, u[0]), (u[1], u[2]), (u[3], u[4])])
     return third_row(rows)
 
 
@@ -198,11 +226,11 @@
 
 def step_kernel(
     gx_count, gy_count,
-    links, momentum, mix_xy, row_part, plane, z_rows, t_rows,
+    links_far, momentum, mix_xy, row_part, plane, z_rows, t_rows,
     out_momentum, out_link,
-    ahead, peer_x, shifted_x, lower, peer_lower, total,
+    links, crossed, coded, ahead, peer_x, shifted_x, lower, peer_lower, total,
     outgoing, gathered, filtered, returned, table_high, table_low, weights,
-    halo_send, halo_recv, peer_send, peer_recv, out_send, out_recv, back_send, back_recv,
+    load_sem, halo_send, halo_recv, peer_send, peer_recv, out_send, out_recv, back_send, back_recv,
 ):
     gx, gy = lax.axis_index("gx"), lax.axis_index("gy")
     parts = gx_count * gy_count
@@ -224,20 +252,47 @@
         return carry
 
     lax.fori_loop(1, parts, greet, 0)
+    loads = [pltpu.make_async_copy(links_far.at[d], links.at[d], load_sem.at[d]) for d in range(4)]
+    for d in (1, 2, 3, 0):
+        loads[d].start()
+
+    def pack(nu):
+        def chunk(j, carry):
+            lanes = pl.ds(pl.multiple_of(j * LANES, LANES), LANES)
+            ref = links.at[nu + 1]
+            rows_of = [
+                [(ref[3 * r + k, :, lanes], ref[6 + 3 * r + k, :, lanes]) for k in range(3)]
+                for r in range(2)
+            ]
+            for index, value in enumerate(encode(rows_of)):
+                coded[nu, index, :, lanes] = value
+            return carry
+
+        loads[nu + 1].wait()
+        lax.fori_loop(0, chunks, chunk, 0)
+
+    half = sites // HALVES
+
+    def halo_copy(nu, piece):
+        lanes = pl.ds(piece * half, half)
+        slot = nu * HALVES + piece
+        return pltpu.make_async_remote_copy(
+            coded.at[nu, :, :, lanes], ahead.at[nu, :, :, lanes],
+            halo_send.at[slot], halo_recv.at[slot], device_id=behind,
+        )
+
+    halo = [[halo_copy(nu, piece) for piece in range(HALVES)] for nu in range(3)]
+    fetch_x = pltpu.make_async_remote_copy(
+        links_far.at[0], peer_x, peer_send.at[0], peer_recv.at[0], device_id=y_before
+    )
+    pack(0)
     pl.semaphore_wait(barrier, parts - 1)
-
-    halo = [
-        pltpu.make_async_remote_copy(
-            links.at[nu + 1], ahead.at[nu], halo_send.at[nu], halo_recv.at[nu], device_id=behind
-        )
-        for nu in range(3)
-    ]
-    fetch_x = pltpu.make_async_remote_copy(
-        links.at[0], peer_x, peer_send.at[0], peer_recv.at[0], device_id=y_before
-    )
+    for nu in range(3):
+        if nu > 0:
+            pack(nu)
+        for copy in halo[nu]:
+            copy.start()
     fetch_x.start()
-    for copy in halo:
-        copy.start()
 
     def make_table(z, carry):
         block = t_rows[...] * z_rows[z]
@@ -250,6 +305,8 @@
     lax.fori_loop(0, NZ, make_table, 0)
     weights[...] = 4.0 / (row_part[...] + plane[me])
 
+    loads[0].wait()
+
     def shift_sides(entry, carry):
         value = links[0, entry]
         shifted_x[1, entry] = move_z(value, -1)
@@ -265,32 +322,56 @@
 
     lax.fori_loop(0, 12, shift_y, 0)
 
-    def direction(nu, first):
+    def cross(nu):
+        def chunk(j, carry):
+            lanes = pl.ds(pl.multiple_of(j * LANES, LANES), LANES)
+            pair = product(load_link(links.at[nu + 1], lanes), load_link(shifted_x.at[nu], lanes))
+            for i in range(3):
+                for k in range(3):
+                    crossed[nu, 3 * i + k, :, lanes] = pair[i][k][0]
+                    crossed[nu, 9 + 3 * i + k, :, lanes] = pair[i][k][1]
+            return carry
+
+        lax.fori_loop(0, chunks, chunk, 0)
+
+    for nu in range(3):
+        cross(nu)
+
+    def direction(nu, piece):
+        per = chunks // HALVES
+
         def chunk(j, carry):
             lanes = pl.ds(pl.multiple_of(j * LANES, LANES), LANES)
             link_nu = load_link(links.at[nu + 1], lanes)
             across = load_link(shifted_x.at[nu], lanes)
-            corner = product(load_link(links.at[0], lanes), load_link(ahead.at[nu], lanes))
-            upper = algebra_parts(corner, adjoint(product(link_nu, across)))
+            corner = product(load_link(links.at[0], lanes), decode([ahead[nu, e, :, lanes] for e in range(10)]))
+            pair = [
+                [
+                    (crossed[nu, 3 * i + k, :, lanes], crossed[nu, 9 + 3 * i + k, :, lanes])
+                    for k in range(3)
+                ]
+                for i in range(3)
+            ]
+            upper = algebra_parts(corner, adjoint(pair))
             below = algebra_parts(product(across, adjoint(corner)), link_nu)
             for a in range(8):
-                total[a, :, lanes] = upper[a] if first else total[a, :, lanes] + upper[a]
+                total[a, :, lanes] = upper[a] if nu == 0 else total[a, :, lanes] + upper[a]
                 lower[nu, a, :, lanes] = below[a]
             return carry
 
-        lax.fori_loop(0, chunks, chunk, 0)
-
-    halo[0].wait()
-    direction(0, True)
+        lax.fori_loop(piece * per, (piece + 1) * per, chunk, 0)
+
     send_lower = pltpu.make_async_remote_copy(
         lower.at[0], peer_lower, peer_send.at[1], peer_recv.at[1], device_id=y_after
     )
-    send_lower.start()
-    halo[1].wait()
-    direction(1, False)
-    send_lower.wait()
-    halo[2].wait()
-    direction(2, False)
+    for nu in range(3):
+        for piece in range(HALVES):
+            halo[nu][piece].wait()
+            direction(nu, piece)
+        if nu == 0:
+            send_lower.start()
+        if nu == 1:
+            send_lower.wait()
 
     def finish(a, carry):
         force = total[a] + move_z(lower[1, a], 1) + move_t(lower[2, a], 1)
@@ -299,13 +380,6 @@
         return carry
 
     lax.fori_loop(0, 8, finish, 0)
-
-    spectrum = plane_transform(out_momentum[...].reshape(colors * rows, sites), table_high, table_low)
-    spectrum = spectrum.reshape(colors, rows, sites)
-    pieces = sites // width
-    for part in range(parts):
-        c, k = part // pieces, part % pieces
-        outgoing[part] = spectrum[c, :, k * width : (k + 1) * width]
 
     def own_rows(index):
         return pl.ds(pl.multiple_of(index * rows, rows), rows)
@@ -316,16 +390,36 @@
             device_id=place(to),
         )
 
-    def start_out(offset, carry):
-        out_copy(lax.rem(me + offset, parts), me).start()
-        return carry
+    pieces = sites // width
+    groups = min(2, pieces)
+    group_sites = sites // groups
+    fields = out_momentum[...].reshape(colors * rows, sites)
+    for group in range(groups):
+        at = slice(group * group_sites, (group + 1) * group_sites)
+        spectrum = plane_transform(fields, table_high.at[:, at], table_low.at[:, at])
+        spectrum = spectrum.reshape(colors, rows, group_sites)
+        own = group * (pieces // groups)
+        for c in range(colors):
+            for k in range(pieces // groups):
+                outgoing[c * pieces + own + k] = spectrum[c, :, k * width : (k + 1) * width]
+
+        def start_out(offset, carry):
+            to = lax.rem(me + offset, parts)
+            kind = lax.rem(to, pieces)
+
+            @pl.when(jnp.logical_and(kind >= own, kind < own + pieces // groups))
+            def _():
+                out_copy(to, me).start()
+
+            return carry
+
+        lax.fori_loop(1, parts, start_out, 0)
 
     def wait_out(offset, carry):
         other = lax.rem(me + offset, parts)
         out_copy(other, other).wait()
         return carry
 
-    lax.fori_loop(1, parts, start_out, 0)
     gathered[own_rows(me), :] = outgoing[me]
     lax.fori_loop(1, parts, wait_out, 0)
 
@@ -404,6 +498,8 @@
     def body(*refs):
         step_kernel(gx_count, gy_count, *refs)
 
+    constants = tables(gx_count * layers, gy_count * rows, colors, parts)
+    grant = 67043328 - 3000 * 1024
     vmem = pl.BlockSpec(memory_space=pltpu.VMEM)
     new_momentum, new_link = pl.pallas_call(
         body,
@@ -411,10 +507,13 @@
             jax.ShapeDtypeStruct((colors, rows, sites), f32),
             jax.ShapeDtypeStruct((12, rows, sites), f32),
         ),
-        in_specs=[vmem] * 7,
+        in_specs=[pl.BlockSpec(memory_space=pltpu.HBM)] + [vmem] * 6,
         out_specs=(vmem, vmem),
         scratch_shapes=[
-            pltpu.VMEM((3, 12, rows, sites), f32),
+            pltpu.VMEM((4, 12, rows, sites), f32),
+            pltpu.VMEM((3, 18, rows, sites), f32),
+            pltpu.VMEM((3, 10, rows, sites), f32),
+            pltpu.VMEM((3, 10, rows, sites), f32),
             pltpu.VMEM((12, rows, sites), f32),
             pltpu.VMEM((3, 12, rows, sites), f32),
             pltpu.VMEM((3, colors, rows, sites), f32),
@@ -427,13 +526,13 @@
             pltpu.VMEM((sites, sites), jnp.bfloat16),
             pltpu.VMEM((sites, sites), jnp.bfloat16),
             pltpu.VMEM((everything, width), f32),
-            dma((3,)), dma((3,)), dma((2,)), dma((2,)),
+            dma((4,)), dma((3 * HALVES,)), dma((3 * HALVES,)), dma((2,)), dma((2,)),
             dma((parts,)), dma((parts,)), dma((parts,)), dma((parts,)),
         ],
         compiler_params=pltpu.CompilerParams(
-            collective_id=0, has_side_effects=True, vmem_limit_bytes=60 * 1024 * 1024
+            collective_id=0, has_side_effects=True, vmem_limit_bytes=grant
         ),
-    )(links, fields, *tables(gx_count * layers, gy_count * rows, colors, parts))
+    )(links, fields, *constants)
     return (new_momentum.reshape(momentum.shape), new_link.reshape((12,) + momentum.shape[1:]))
 
 

time: 59 us -> 52.6 us (0.89)
  Pallas kernels: 54.7 us -> 48.3 us
    pallas_call x1, Pallas kernels: 54.7 us -> 48.3 us  [shards(): pl.pallas_call(body, out_shape=(jax.ShapeDtypeStruct((colors, rows, sites...]
where the time goes in v1:
time: 52.6 us; the launch traced here: 52.4 us
  Pallas kernels  48.3 us (92%)
  local copies, waits for them, and re-layouts  3.44 us (7%)
  between operations  0.64 us (1%)
    pallas_call x1, Pallas kernels, shards(): pl.pallas_call(body, out_shape=(jax.ShapeDtypeStruct((colors, rows, sites...  48.3 us
    unnamed x2, local copies, waits for them, and re-layouts  3.44 us

profile of v1, /device:TPU:0, one launch (start us, length us, event | category | flops | bytes accessed | tf_op | source)
XLA Modules:
  0.0 52.4 jit_solution(8458226203676521056)
XLA Ops:
  0.6 48.3 %shard_map.86 = (f32[8,8,1024]{2,1,0:T(8,128)}, f32[12,8,1024]{2,1,0:T(8,128)}) custom-call(f32[4,12,8,1024]{3,2,1,0:T(8,128)} %bitcast.8, f32[8,8,1024]{2,1,0:T(8,128)} %bitcast.10, f32[128,128]{1,0:T(8,128)} %constant.10.clone.refs_2_, f32[128,1]{1,0:T(8,128)} %constant.11.clone.refs_3_, f32[16,1,512]{2,1,0:T(1,128)} %constant.12.clone.refs_4_, ...), custom_call_target="tpu_custom_call" | custom-call | tf_op jit(solution)/shard_map/pallas_call | solution.py:504
  49.0 1.7 %copy.13 = f32[8,1,8,1024]{3,2,1,0:T(8,128)} copy(f32[8,1,8,1024]{3,2,1,0:T(8,128)} %bitcast.11) | data formatting | bytes 524288
  50.6 1.8 %copy.14 = f32[12,1,8,1024]{3,2,1,0:T(8,128)} copy(f32[12,1,8,1024]{3,2,1,0:T(8,128)} %bitcast.9) | data formatting | bytes 786432
